TPU v7x, 256 devices: a whole 4x4x8 slice. The times are simulated.
256 devices in a mesh: batch: 16 (over z, core), vocab: 16 (over y, x).
Axes of the slice: x: 4, y: 4, z: 8, core: 2. Of those that a mesh axis runs over, the one named last changes fastest.
Arguments:
- hidden: bfloat16 [2048, 4096], P('batch'), may hold values from -40 to 40
- exit_layer: int32 [2048], P('batch'), may hold values from 0 to 7
- exit_gains: float32 [8, 4096], replicated, may hold values from 0.1 to 1.9
- unembed: bfloat16 [4096, 128256], P(None, ('batch', 'vocab')), may hold values from -10 to 10
- targets: int32 [2048], replicated, may hold values from 0 to 128255
- values: float32 [2048], P('batch'), may hold values from -6 to 6
- rewards: float32 [2048], P('batch'), may hold values from -2 to 2
- ref_logprob: float32 [2048], P('batch'), may hold values from -16 to -6
- segment_end: int32 [2048], P('batch'), may hold values 0 or 1
Outputs:
- logprob: float32 [2048], P('batch')
- advantages: float32 [2048], P('batch')
All inputs are finite; a program needn't handle non-finite values. No bound on the sum of `segment_end` on one device may be relied on, other than what follows from the above.
Results may differ from a plain program's by a relative error of at most 0.00054.
Values may be sent and summed in bfloat16 or wider, within the bound.
A program may use at most 128 MiB of HBM per device.

v0:
```python
import jax
import jax.numpy as jnp
from jax import lax
from jax.sharding import Mesh
from jax.sharding import PartitionSpec as P

BATCH_VOCAB = ("batch", "vocab_0", "vocab_1")
VOCAB = ("vocab_0", "vocab_1")
epsilon_norm = 1e-05
discount = 1.0
trace_decay = 0.999
penalty_weight = 0.1


def gathered_once(shard, axis):
    leaves = jax.tree.leaves(shard)
    sequence = sorted(range(len(leaves)), key=lambda k: -leaves[k].size)
    width = (1, *leaves[sequence[0]].shape)[-1]
    lines = [
        jnp.pad(leaves[k].reshape(-1), (0, -leaves[k].size % width)).reshape(-1, width)
        for k in sequence
    ]
    both, at, found = (lax.all_gather(jnp.concatenate(lines), axis), 0, {})
    for k, line in zip(sequence, lines):
        piece = both[:, at : at + len(line)].reshape(len(both), -1)
        found[k] = piece[:, : leaves[k].size].reshape(-1, *leaves[k].shape)
        at += len(line)
    numbers = iter(range(len(leaves)))
    return jax.tree.map(lambda _: found[next(numbers)], shard)


def joined_all(shard, axes, combine):
    for axis in axes:
        pieces = gathered_once(shard, axis)
        shard = jax.tree.map(lambda part: part[0], pieces)
        for k in range(1, lax.axis_size(axis)):
            shard = combine(shard, jax.tree.map(lambda part: part[k], pieces))
    return shard


def from_behind(value, axis, steps):
    count = lax.axis_size(axis)
    initial, last = (max(0, -steps), min(count, count - steps))
    return lax.ppermute(value, axis, [(source, source + steps) for source in range(initial, last)])


def from_everyone(shard, axis):
    length = lax.axis_size(axis)
    return lax.all_to_all(
        jnp.broadcast_to(shard[None], (length, *shard.shape)), axis, 0, 0, tiled=True
    )


def gathered_once_2(shard, axis):
    leaves = jax.tree.leaves(shard)
    sequence = sorted(range(len(leaves)), key=lambda k: -leaves[k].size)
    width = (1, *leaves[sequence[0]].shape)[-1]
    lines = [
        jnp.pad(leaves[k].reshape(-1), (0, -leaves[k].size % width)).reshape(-1, width)
        for k in sequence
    ]
    both, at, found = (from_everyone(jnp.concatenate(lines), axis), 0, {})
    for k, line in zip(sequence, lines):
        piece = both[:, at : at + len(line)].reshape(len(both), -1)
        found[k] = piece[:, : leaves[k].size].reshape(-1, *leaves[k].shape)
        at += len(line)
    numbers = iter(range(len(leaves)))
    return jax.tree.map(lambda _: found[next(numbers)], shard)


def collected_alike(shard, axis):
    leaves, found = (jax.tree.leaves(shard), {})
    for initial, a in enumerate(leaves):
        if initial not in found:
            alike = [k for k, b in enumerate(leaves) if b.dtype == a.dtype]
            got = (
                gathered_once_2([leaves[k] for k in alike], axis)
                if len(alike) > 1
                else [from_everyone(a, axis)]
            )
            for k, b in zip(alike, got):
                found[k] = b
    numbers = iter(range(len(leaves)))
    return jax.tree.map(lambda _: found[next(numbers)], shard)


def joined_by_halves(pieces, combine):
    while len(jax.tree.leaves(pieces)[0]) > 1:
        pieces = jax.vmap(combine)(
            *(jax.tree.map(lambda part: part[side::2], pieces) for side in (0, 1))
        )
    return jax.tree.map(lambda part: part[0], pieces)


def prefix(shard, axis, combine, identity):
    length, mine = (lax.axis_size(axis), lax.axis_index(axis))
    passed = jnp.arange(length) > mine

    def kept(part, zero, own):
        part = jnp.where(
            passed.reshape(-1, *(1 for _ in own.shape)), part, jnp.asarray(zero, own.dtype)
        )
        return part[::-1]

    pieces = collected_alike(shard, axis)
    return joined_by_halves(jax.tree.map(kept, pieces, identity, shard), combine)


def normalize(rows, layers, exit_gains):
    states = rows.astype(jnp.float32)
    inverse = lax.rsqrt(jnp.mean(states * states, axis=-1, keepdims=True) + epsilon_norm)
    selector = (
        layers[:, None] == jnp.arange(exit_gains.shape[0], dtype=jnp.int32)[None, :]
    ).astype(jnp.float32)
    scaling = jnp.dot(selector, exit_gains, precision=lax.Precision.HIGHEST)
    return (states * inverse * scaling).astype(jnp.bfloat16)


def per_device(
    hidden, exit_layer, exit_gains, unembed, targets, values, rewards, ref_logprob, segment_end
):
    column_count = unembed.shape[1]
    column_start = lax.axis_index(BATCH_VOCAB) * column_count
    columns = jnp.arange(column_count, dtype=jnp.int32)
    total_rows = targets.shape[0]
    owned = hidden.shape[0]
    peers = lax.axis_size("batch")
    width = hidden.shape[1]
    share = owned // lax.axis_size(VOCAB)
    first_row = lax.axis_index(VOCAB) * share
    own_rows = lax.dynamic_slice_in_dim(hidden, first_row, share, 0)
    own_layers = lax.dynamic_slice_in_dim(exit_layer, first_row, share, 0)
    normed = normalize(own_rows, own_layers, exit_gains)
    gathered = lax.all_gather(normed, BATCH_VOCAB, axis=0, tiled=True)
    block_rows = 512
    block_count = total_rows // block_rows

    def score_block(pair):
        rows_block, ids_block = pair
        logits = jnp.dot(rows_block, unembed, preferred_element_type=jnp.float32)
        row_max = jnp.max(logits, axis=1)
        row_total = jnp.sum(jnp.exp(logits - row_max[:, None]), axis=1)
        wanted = ids_block - column_start
        picked = jnp.sum(jnp.where(columns[None, :] == wanted[:, None], logits, 0.0), axis=1)
        return (row_max, row_total, picked)

    maxima, totals, picks = lax.map(
        score_block,
        (
            gathered.reshape(block_count, block_rows, width),
            targets.reshape(block_count, block_rows),
        ),
    )
    maxima = maxima.reshape(total_rows)
    totals = totals.reshape(total_rows)
    picks = picks.reshape(total_rows)
    maxima, totals, picks = (
        lax.all_to_all(maxima, "batch", split_axis=0, concat_axis=0, tiled=True),
        lax.all_to_all(totals, "batch", split_axis=0, concat_axis=0, tiled=True),
        lax.all_to_all(picks, "batch", split_axis=0, concat_axis=0, tiled=True),
    )
    maxima = maxima.reshape(peers, owned)
    totals = totals.reshape(peers, owned)
    picks = picks.reshape(peers, owned)
    group_max = jnp.max(maxima, axis=0)
    group_total = jnp.sum(totals * jnp.exp(maxima - group_max[None, :]), axis=0)
    group_pick = jnp.sum(picks, axis=0)

    def combine_groups(first, second):
        larger = jnp.maximum(first[0], second[0])
        summed = first[1] * jnp.exp(first[0] - larger) + second[1] * jnp.exp(second[0] - larger)
        return (larger, summed, first[2] + second[2])

    overall_max, overall_total, overall_pick = joined_all(
        (group_max, group_total, group_pick), VOCAB, combine_groups
    )
    logprob = overall_pick - (overall_max + jnp.log(overall_total))
    following = from_behind(values[:1], "batch", -1)
    next_values = jnp.concatenate([values[1:], following])
    keeping = 1.0 - segment_end.astype(jnp.float32)
    shaped = rewards - penalty_weight * (logprob - ref_logprob)
    deltas = shaped + discount * next_values * keeping - values
    factors = discount * trace_decay * keeping

    def backward(running, inputs):
        factor, delta = inputs
        accrued = delta + factor * running[0]
        product = factor * running[1]
        return ((accrued, product), (accrued, product))

    finished, outputs = lax.scan(
        backward,
        (jnp.zeros((), jnp.float32), jnp.ones((), jnp.float32)),
        (factors, deltas),
        reverse=True,
    )
    local_adv, products = outputs
    head_adv = local_adv[:1]
    head_prod = products[:1]

    def compose(earlier, later):
        return (later[0] * earlier[0], later[1] + later[0] * earlier[1])

    composed, incoming = prefix(
        (head_prod, head_adv),
        "batch",
        compose,
        (jnp.ones((1,), jnp.float32), jnp.zeros((1,), jnp.float32)),
    )
    advantages = local_adv + products * incoming
    return (logprob, advantages)


def solution(mesh):
    torus = Mesh(mesh.devices.reshape(mesh.shape["batch"], 4, 4), ("batch", "vocab_0", "vocab_1"))
    return jax.shard_map(
        per_device,
        mesh=torus,
        in_specs=(
            P("batch", None),
            P("batch"),
            P(),
            P(None, BATCH_VOCAB),
            P(),
            P("batch"),
            P("batch"),
            P("batch"),
            P("batch"),
        ),
        out_specs=(P("batch"), P("batch")),
        check_vma=False,
    )
```

profile of v0, /device:TPU:1, one launch (start us, length us, event | category | flops | bytes accessed | tf_op | source)
XLA Modules:
  0.0 654.8 jit_solution(7538724835867573216)
XLA Ops:
  7.2 1.0 fusion.7
  8.2 0.7 dynamic_slice.34
  9.0 1.7 fusion.6
  10.8 0.7 reshape.381
  11.5 129.7 %all-gather.6.cloned.1.call-done = bf16[2048,4096]{1,0:T(8,128)(2,1)} async-done(((bf16[8,4096]{1,0:T(8,128)(2,1)}), bf16[2048,4096]{1,0:T(8,128)(2,1)}) %all-gather.6.cloned.1.call-update) | async-done | bytes 16777232 | tf_op jit(solution)/shard_map/all_gather | solution.py:134
  141.2 25.1 %while.36 = (s32[]{:T(128)}, f32[4,512]{1,0:T(4,128)S(1)}, f32[4,512]{1,0:T(4,128)S(1)}, f32[4,512]{1,0:T(4,128)S(1)}, bf16[4,512,4096]{2,1,0:T(8,128)(2,1)}, /*...) while((s32[]{:T(128)}, f32[4,512]{1,0:T(4,128)S(1)}, ...), condition=%wide.region_5.6_spmd.clone, body=%wide.region_1.5_spmd.clone.sunk | while | flops 2102884352 | bytes 10402425 | solution.py:147
  141.2 5.8 fusion.51
  147.5 5.8 fusion.51
  153.7 5.8 fusion.51
  160.0 5.8 fusion.51
  166.9 4.6 all-to-all-start
  172.1 6.4 all-to-all-done
  178.5 3.9 all-to-all-start.1
  182.4 2.1 collective-permute-start
  185.2 4.2 all-to-all-done.1
  189.4 3.9 all-to-all-start.2
  193.4 7.1 %all-to-all-done.2 = f32[16,128,1]{1,2,0:T(1,128)S(1)} async-done(((f32[16,128,1]{1,2,0:T(1,128)}), f32[16,128,1]{1,2,0:T(1,128)S(1)}, u32[]{:S(2)}, u32[]{:S(2)}) %all-to-all-start.2) | async-done | bytes 8224 | tf_op jit(solution)/shard_map/all_to_all | solution.py:160
  200.5 8.5 %all-gather.2 = f32[4,3,128]{2,1,0:T(4,128)S(1)} all-gather(f32[1,3,128]{2,1,0:T(4,128)S(1)} %maximum_bitcast_fusion), channel_id=2, replica_groups=mesh['batch'=16,'vocab_0'=4,'vocab_1'=4] {'vocab_0'}, dimensions={0}, use_global_device_ids=true | all-gather | bytes 7680 | tf_op jit(solution)/shard_map/all_gather | solution.py:23
  209.1 8.1 %all-gather.3 = f32[4,3,128]{2,1,0:T(4,128)S(1)} all-gather(f32[1,3,128]{2,1,0:T(4,128)S(1)} %maximum_bitcast_fusion.1), channel_id=3, replica_groups=mesh['batch'=16,'vocab_0'=4,'vocab_1'=4] {'vocab_1'}, dimensions={0}, use_global_device_ids=true | all-gather | bytes 7680 | tf_op jit(solution)/shard_map/all_gather | solution.py:23
  217.2 1.2 fusion.31
  218.4 408.9 %while.35 = (s32[]{:T(128)}, f32[]{:T(128)}, f32[]{:T(128)}, f32[128]{0:T(128)S(1)}, f32[128]{0:T(128)S(1)}, /*index=5*/f32[128]{0:T(128)S(1)}, f32[128]{0:T(128)S(1)}, s32[]{:T(128)}, s32[]{:T(128)}) while((s32[]{:T(128)}, f32[]{:T(128)}, f32[]{:T(128)}, f32[128]{0:T(128)S(1)}, f32[128]{0:T(128)S(1)}, /*index=5*/f32[128]{0:T(128)S(1)}, ...), condition=%wide.region_10.11_spmd, body=%wide.region_9.10_spmd.sunk | while | flops 6 | bytes 189 | solution.py:191
  219.5 0.6 dynamic_slice.50
  222.7 0.6 dynamic_slice.50
  225.9 0.6 dynamic_slice.50
  229.1 0.6 dynamic_slice.50
  232.3 0.6 dynamic_slice.50
  235.5 0.6 dynamic_slice.50
  238.7 0.6 dynamic_slice.50
  241.9 0.6 dynamic_slice.50
  245.1 0.6 dynamic_slice.50
  248.3 0.6 dynamic_slice.50
  251.5 0.6 dynamic_slice.50
  254.7 0.6 dynamic_slice.50
  257.9 0.6 dynamic_slice.50
  261.1 0.6 dynamic_slice.50
  264.3 0.6 dynamic_slice.50
  267.5 0.6 dynamic_slice.50
  270.6 0.6 dynamic_slice.50
  273.8 0.6 dynamic_slice.50
  277.0 0.6 dynamic_slice.50
  280.2 0.6 dynamic_slice.50
  283.4 0.6 dynamic_slice.50
  286.6 0.6 dynamic_slice.50
  289.8 0.6 dynamic_slice.50
  293.0 0.6 dynamic_slice.50
  296.2 0.6 dynamic_slice.50
  299.4 0.6 dynamic_slice.50
  312.2 0.6 dynamic_slice.50
  334.5 0.6 dynamic_slice.50
  353.7 0.6 dynamic_slice.50
  372.9 0.6 dynamic_slice.50
  395.2 0.6 dynamic_slice.50
  414.4 0.6 dynamic_slice.50
  433.6 0.6 dynamic_slice.50
  455.9 0.6 dynamic_slice.50
  475.1 0.6 dynamic_slice.50
  494.3 0.6 dynamic_slice.50
  516.6 0.6 dynamic_slice.50
  535.8 0.6 dynamic_slice.50
  555.0 0.6 dynamic_slice.50
  577.3 0.6 dynamic_slice.50
  596.5 0.6 dynamic_slice.50
  615.7 0.6 dynamic_slice.50
  627.4 15.1 %all_to_all.32 = f32[16,2,1]{1,2,0:T(1,128)S(1)} all-to-all(f32[16,2,1]{1,2,0:T(1,128)S(1)} %broadcast_in_dim.56), channel_id=1, replica_groups=mesh['batch'=16,'vocab_0'=4,'vocab_1'=4] {'batch'}, dimensions={0} | all-to-all | bytes 256 | tf_op jit(solution)/shard_map/all_to_all | solution.py:49
  (546 shorter events, 163.6 us)
Async XLA Ops:
  7.2 1.8 copy-start
  7.2 134.0 %all-gather.6.cloned.1.call-start = ((), (), s32[]{:S(2)}) async-start(), calls=%async_computation.4 | async-start | bytes 16842752 | tf_op jit(solution)/shard_map/all_gather | solution.py:134
  141.2 41.2 %copy-start.1 = (f32[128]{0:T(128)S(1)}, f32[128]{0:T(128)}, u32[]{:S(2)}) copy-start(f32[128]{0:T(128)} %param.18) | copy-start | bytes 1540
  141.2 76.1 %copy-start.2 = (f32[128]{0:T(128)S(1)}, f32[128]{0:T(128)}, u32[]{:S(2)}) copy-start(f32[128]{0:T(128)} %param.19) | copy-start | bytes 1540
  141.2 76.1 %copy-start.3 = (f32[128]{0:T(128)S(1)}, f32[128]{0:T(128)}, u32[]{:S(2)}) copy-start(f32[128]{0:T(128)} %param.20) | copy-start | bytes 1540
  141.2 76.1 %copy-start.4 = (s32[128]{0:T(128)S(1)}, s32[128]{0:T(128)}, u32[]{:S(2)}) copy-start(s32[128]{0:T(128)} %param.21) | copy-start | bytes 1540
  166.9 11.6 %all-to-all-start = ((f32[16,128,1]{1,2,0:T(1,128)}), f32[16,128,1]{1,2,0:T(1,128)S(1)}, u32[]{:S(2)}, u32[]{:S(2)}) async-start(f32[16,128,1]{1,2,0:T(1,128)} %all_to_all.21), calls=%async_computation | async-start | bytes 16384 | tf_op jit(solution)/shard_map/all_to_all | solution.py:158
  178.5 10.9 %all-to-all-start.1 = ((f32[16,128,1]{1,2,0:T(1,128)}), f32[16,128,1]{1,2,0:T(1,128)S(1)}, u32[]{:S(2)}, u32[]{:S(2)}) async-start(f32[16,128,1]{1,2,0:T(1,128)} %all_to_all.23), calls=%async_computation.1 | async-start | bytes 16384 | tf_op jit(solution)/shard_map/all_to_all | solution.py:159
  182.4 34.8 %collective-permute-start = (f32[1]{0:T(128)S(1)}, f32[1]{0:T(128)}, u32[]{:S(2)}, u32[]{:S(2)}) collective-permute-start(f32[1]{0:T(128)S(1)} %bitcast.211), channel_id=1, source_target_pairs={{16,0},{32,16},{48,32},{64,48},{80,64},{96,80},{112,96},{128,112},... | collective-permute-start | bytes 20 | tf_op jit(solution)/shard_map/ppermute | solution.py:44
  189.4 11.0 %all-to-all-start.2 = ((f32[16,128,1]{1,2,0:T(1,128)}), f32[16,128,1]{1,2,0:T(1,128)S(1)}, u32[]{:S(2)}, u32[]{:S(2)}) async-start(f32[16,128,1]{1,2,0:T(1,128)} %all_to_all.25), calls=%async_computation.2 | async-start | bytes 16384 | tf_op jit(solution)/shard_map/all_to_all | solution.py:160
Sparse Core Ops, SparseCore 0:
  11.7 129.4 all-gather.5
where the time goes:
time: 662 us; the launch traced here: 655 us
  loops' own time  227 us (34%)
  local copies, waits for them, and re-layouts  189 us (29%)
  waiting for transfers between devices  147 us (22%)
  blocking collectives  31.8 us (5%)
  matrix products  24.9 us (4%)
  between operations  16 us (2%)
  starting transfers between devices  14.5 us (2%)
    another operation x1, loops' own time, per_device(): lax.scan(backward, (jnp.zeros((), jnp.float32), jnp.ones((), jnp.float32)...  227 us
    dynamic_slice x256, local copies, waits for them, and re-layouts, per_device(): lax.scan(backward, (jnp.zeros((), jnp.float32), jnp.ones((), jnp.float32)...  152 us
    all_gather x1, waiting for transfers between devices, per_device(): gathered = lax.all_gather(normed, BATCH_VOCAB, axis=0, tiled=True)  130 us
    dynamic_update_slice x256, local copies, waits for them, and re-layouts, per_device(): lax.scan(backward, (jnp.zeros((), jnp.float32), jnp.ones((), jnp.float32)...  29.4 us
    dot_general x4, matrix products, score_block(): logits = jnp.dot(rows_block, unembed, preferred_element_type=jnp.float32)  23.2 us
    all_gather x2, blocking collectives, gathered_once(): both, at, found = (lax.all_gather(jnp.concatenate(lines), axis), 0, {})  16.7 us
    all_to_all x1, blocking collectives, from_everyone(): lax.all_to_all(jnp.broadcast_to(shard[None], (length, *shard.shape)), axi...  15.1 us
  transfers between devices with their start and end apart: 5, of which 4 were waited for; matrix products, arithmetic and copies ran while one was open for 0% of the time, Pallas kernels for 0%

commit v1 on v0

--- a/solution.py
+++ b/solution.py
@@ -131,7 +131,9 @@
     own_rows = lax.dynamic_slice_in_dim(hidden, first_row, share, 0)
     own_layers = lax.dynamic_slice_in_dim(exit_layer, first_row, share, 0)
     normed = normalize(own_rows, own_layers, exit_gains)
-    gathered = lax.all_gather(normed, BATCH_VOCAB, axis=0, tiled=True)
+    tile_out = jnp.stack([normed for _ in range(lax.axis_size(BATCH_VOCAB))], 0)
+    side_arr = lax.all_to_all(tile_out, BATCH_VOCAB, split_axis=0, concat_axis=0)
+    gathered = jnp.concatenate(side_arr, 0)
     block_rows = 512
     block_count = total_rows // block_rows
 

time: 662 us -> 905 us (1.37)
  waiting for transfers between devices: 147 us -> 382 us
  starting transfers between devices: 14.5 us -> 31.4 us
  between operations: 16 us -> 2.63 us
    all_to_all x0 -> x1, waiting for transfers between devices: none -> 365 us  [per_device(): lax.all_to_all(tile_out, BATCH_VOCAB, split_axis=0, concat_axis=0)]
    all_gather x1 -> x0, waiting for transfers between devices: 130 us -> none  [per_device(): gathered = lax.all_gather(normed, BATCH_VOCAB, axis=0, tiled=True)]
    all_to_all x0 -> x1, starting transfers between devices: none -> 16.6 us  [per_device(): lax.all_to_all(tile_out, BATCH_VOCAB, split_axis=0, concat_axis=0)]
where the time goes in v1:
time: 905 us; the launch traced here: 898 us
  waiting for transfers between devices  382 us (42%)
  loops' own time  227 us (25%)
  local copies, waits for them, and re-layouts  194 us (21%)
  blocking collectives  31.6 us (3%)
  starting transfers between devices  31.4 us (3%)
  matrix products  24.3 us (3%)
    all_to_all x1, waiting for transfers between devices, per_device(): lax.all_to_all(tile_out, BATCH_VOCAB, split_axis=0, concat_axis=0)  365 us
    another operation x1, loops' own time, per_device(): lax.scan(backward, (jnp.zeros((), jnp.float32), jnp.ones((), jnp.float32)...  227 us
    dynamic_slice x256, local copies, waits for them, and re-layouts, per_device(): lax.scan(backward, (jnp.zeros((), jnp.float32), jnp.ones((), jnp.float32)...  152 us
    dynamic_update_slice x256, local copies, waits for them, and re-layouts, per_device(): lax.scan(backward, (jnp.zeros((), jnp.float32), jnp.ones((), jnp.float32)...  29.4 us
    dot_general x4, matrix products, score_block(): logits = jnp.dot(rows_block, unembed, preferred_element_type=jnp.float32)  23.2 us
  transfers between devices with their start and end apart: 5, of which 4 were waited for; matrix products, arithmetic and copies ran while one was open for 0% of the time, Pallas kernels for 0%

profile of v1, /device:TPU:1, one launch (start us, length us, event | category | flops | bytes accessed | tf_op | source)
XLA Modules:
  0.0 897.8 jit_solution(14529282053001577024)
XLA Ops:
  0.7 1.0 fusion.7
  1.7 0.7 dynamic_slice.34
  2.4 1.1 fusion.6
  3.5 6.0 stack.2
  9.5 16.6 %all-to-all-start = ((bf16[256,8,4096]{2,1,0:T(8,128)(2,1)}), bf16[256,8,4096]{2,1,0:T(8,128)(2,1)}, u32[]{:S(2)}, u32[]{:S(2)}) async-start(bf16[256,8,4096]{2,1,0:T(8,128)(2,1)} %stack.2), calls=%async_computation | async-start | bytes 33554432 | tf_op jit(solution)/shard_map/all_to_all | solution.py:135
  26.2 364.6 %all-to-all-done = bf16[256,8,4096]{2,1,0:T(8,128)(2,1)} async-done(((bf16[256,8,4096]{2,1,0:T(8,128)(2,1)}), bf16[256,8,4096]{2,1,0:T(8,128)(2,1)}, u32[]{:S(2)}, u32[]{:S(2)}) %all-to-all-start) | async-done | bytes 16777248 | tf_op jit(solution)/shard_map/all_to_all | solution.py:135
  390.8 25.1 %while.36 = (s32[]{:T(128)}, f32[4,512]{1,0:T(4,128)S(1)}, f32[4,512]{1,0:T(4,128)S(1)}, f32[4,512]{1,0:T(4,128)S(1)}, bf16[4,512,4096]{2,1,0:T(8,128)(2,1)}, /*...) while((s32[]{:T(128)}, f32[4,512]{1,0:T(4,128)S(1)}, ...), condition=%wide.region_5.6_spmd.clone, body=%wide.region_1.5_spmd.clone.sunk | while | flops 2102884352 | bytes 10402425 | solution.py:149
  390.8 5.8 fusion.51
  397.1 5.8 fusion.51
  403.4 5.8 fusion.51
  409.7 5.8 fusion.51
  416.5 4.9 all-to-all-start.1
  422.0 6.4 all-to-all-done.1
  428.4 3.9 all-to-all-start.2
  432.3 2.1 collective-permute-start
  435.2 4.2 all-to-all-done.2
  439.4 3.9 all-to-all-start.3
  443.3 7.1 all-to-all-done.3
  450.4 8.4 all-gather.2
  458.9 8.1 all-gather.3
  467.0 1.2 fusion.31
  468.2 408.9 %while.35 = (s32[]{:T(128)}, f32[]{:T(128)}, f32[]{:T(128)}, f32[128]{0:T(128)S(1)}, f32[128]{0:T(128)S(1)}, /*index=5*/f32[128]{0:T(128)S(1)}, f32[128]{0:T(128)S(1)}, s32[]{:T(128)}, s32[]{:T(128)}) while((s32[]{:T(128)}, f32[]{:T(128)}, f32[]{:T(128)}, f32[128]{0:T(128)S(1)}, f32[128]{0:T(128)S(1)}, /*index=5*/f32[128]{0:T(128)S(1)}, ...), condition=%wide.region_10.11_spmd, body=%wide.region_9.10_spmd.sunk | while | flops 6 | bytes 189 | solution.py:193
  469.3 0.6 dynamic_slice.50
  472.5 0.6 dynamic_slice.50
  475.7 0.6 dynamic_slice.50
  478.9 0.6 dynamic_slice.50
  482.1 0.6 dynamic_slice.50
  485.3 0.6 dynamic_slice.50
  488.5 0.6 dynamic_slice.50
  491.7 0.6 dynamic_slice.50
  494.9 0.6 dynamic_slice.50
  498.1 0.6 dynamic_slice.50
  501.3 0.6 dynamic_slice.50
  504.5 0.6 dynamic_slice.50
  507.7 0.6 dynamic_slice.50
  510.9 0.6 dynamic_slice.50
  514.0 0.6 dynamic_slice.50
  517.2 0.6 dynamic_slice.50
  520.4 0.6 dynamic_slice.50
  523.6 0.6 dynamic_slice.50
  526.8 0.6 dynamic_slice.50
  530.0 0.6 dynamic_slice.50
  533.2 0.6 dynamic_slice.50
  536.4 0.6 dynamic_slice.50
  539.6 0.6 dynamic_slice.50
  542.8 0.6 dynamic_slice.50
  549.2 0.6 dynamic_slice.50
  568.4 0.6 dynamic_slice.50
  590.7 0.6 dynamic_slice.50
  609.9 0.6 dynamic_slice.50
  629.1 0.6 dynamic_slice.50
  651.4 0.6 dynamic_slice.50
  670.6 0.6 dynamic_slice.50
  689.8 0.6 dynamic_slice.50
  712.1 0.6 dynamic_slice.50
  731.3 0.6 dynamic_slice.50
  750.5 0.6 dynamic_slice.50
  772.8 0.6 dynamic_slice.50
  792.0 0.6 dynamic_slice.50
  811.2 0.6 dynamic_slice.50
  833.5 0.6 dynamic_slice.50
  852.7 0.6 dynamic_slice.50
  871.9 0.6 dynamic_slice.50
  877.2 15.1 %all_to_all.37 = f32[16,2,1]{1,2,0:T(1,128)S(1)} all-to-all(f32[16,2,1]{1,2,0:T(1,128)S(1)} %broadcast_in_dim.56), channel_id=1, replica_groups=mesh['batch'=16,'vocab_0'=4,'vocab_1'=4] {'batch'}, dimensions={0} | all-to-all | bytes 256 | tf_op jit(solution)/shard_map/all_to_all | solution.py:49
  (548 shorter events, 164.2 us)
Async XLA Ops:
  0.6 1.8 copy-start
  9.5 16.7 %copy-start.1 = (s32[2048]{0:T(1024)S(1)}, s32[2048]{0:T(1024)}, u32[]{:S(2)}) copy-start(s32[2048]{0:T(1024)} %param.17) | copy-start | bytes 24580
  9.5 381.3 %all-to-all-start = ((bf16[256,8,4096]{2,1,0:T(8,128)(2,1)}), bf16[256,8,4096]{2,1,0:T(8,128)(2,1)}, u32[]{:S(2)}, u32[]{:S(2)}) async-start(bf16[256,8,4096]{2,1,0:T(8,128)(2,1)} %stack.2), calls=%async_computation | async-start | bytes 33554432 | tf_op jit(solution)/shard_map/all_to_all | solution.py:135
  390.8 41.5 %copy-start.2 = (f32[128]{0:T(128)S(1)}, f32[128]{0:T(128)}, u32[]{:S(2)}) copy-start(f32[128]{0:T(128)} %param.18) | copy-start | bytes 1540
  390.8 76.2 %copy-start.3 = (f32[128]{0:T(128)S(1)}, f32[128]{0:T(128)}, u32[]{:S(2)}) copy-start(f32[128]{0:T(128)} %param.19) | copy-start | bytes 1540
  390.8 76.2 %copy-start.4 = (f32[128]{0:T(128)S(1)}, f32[128]{0:T(128)}, u32[]{:S(2)}) copy-start(f32[128]{0:T(128)} %param.20) | copy-start | bytes 1540
  390.8 76.2 %copy-start.5 = (s32[128]{0:T(128)S(1)}, s32[128]{0:T(128)}, u32[]{:S(2)}) copy-start(s32[128]{0:T(128)} %param.21) | copy-start | bytes 1540
  416.5 11.9 %all-to-all-start.1 = ((f32[16,128,1]{1,2,0:T(1,128)}), f32[16,128,1]{1,2,0:T(1,128)S(1)}, u32[]{:S(2)}, u32[]{:S(2)}) async-start(f32[16,128,1]{1,2,0:T(1,128)} %all_to_all.25), calls=%async_computation.1 | async-start | bytes 16384 | tf_op jit(solution)/shard_map/all_to_all | solution.py:160
  428.4 10.9 %all-to-all-start.2 = ((f32[16,128,1]{1,2,0:T(1,128)}), f32[16,128,1]{1,2,0:T(1,128)S(1)}, u32[]{:S(2)}, u32[]{:S(2)}) async-start(f32[16,128,1]{1,2,0:T(1,128)} %all_to_all.27), calls=%async_computation.2 | async-start | bytes 16384 | tf_op jit(solution)/shard_map/all_to_all | solution.py:161
  432.3 34.7 %collective-permute-start = (f32[1]{0:T(128)S(1)}, f32[1]{0:T(128)}, u32[]{:S(2)}, u32[]{:S(2)}) collective-permute-start(f32[1]{0:T(128)S(1)} %bitcast.211), channel_id=1, source_target_pairs={{16,0},{32,16},{48,32},{64,48},{80,64},{96,80},{112,96},{128,112},... | collective-permute-start | bytes 20 | tf_op jit(solution)/shard_map/ppermute | solution.py:44
  439.4 11.0 %all-to-all-start.3 = ((f32[16,128,1]{1,2,0:T(1,128)}), f32[16,128,1]{1,2,0:T(1,128)S(1)}, u32[]{:S(2)}, u32[]{:S(2)}) async-start(f32[16,128,1]{1,2,0:T(1,128)} %all_to_all.29), calls=%async_computation.3 | async-start | bytes 16384 | tf_op jit(solution)/shard_map/all_to_all | solution.py:162
